TPU v7x, 32 devices: a whole 2x2x4 slice. The times are simulated.
32 devices in a mesh: row: 4 (over y, x), col: 8 (over z, core).
Axes of the slice: x: 2, y: 2, z: 4, core: 2. Of those that a mesh axis runs over, the one named last changes fastest.
Arguments:
- pair_rep: bfloat16 [96, 96, 128], P('row', 'col'), may hold values from -6 to 6
- pair_mask: int32 [96, 96], P('row', 'col'), may hold values 0 or 1
- proj_weight: bfloat16 [2, 5, 128, 128], replicated, may hold values from -0.5 to 0.5
- out_weight: bfloat16 [2, 128, 128], replicated, may hold values from -0.5 to 0.5
- norm_gain: float32 [2, 2, 128], replicated, may hold values from 0.25 to 1.75
- norm_bias: float32 [2, 2, 128], replicated, may hold values from -1.5 to 1.5
Outputs:
- pair_out: bfloat16 [96, 96, 128], P('row', 'col')
Inputs may be any that keep to these rules, and one draw needn't show every extreme that they name: pair_mask holds only 0 and 1.
All inputs are finite; a program needn't handle non-finite values.
Results may differ from a plain program's by a relative error of at most 0.0095.
Values may be sent and summed in bfloat16 or wider, within the bound.
A program may use at most 64 MiB of HBM per device.

v0:
```python
import jax
import jax.numpy as jnp
from jax import lax
from jax.sharding import PartitionSpec as P

epsilon = 1e-05


def scattered(term, extent, axis):
    whole = term(jnp.int32(0), extent * lax.axis_size(axis))
    return lax.psum_scatter(whole, axis, scatter_dimension=0, tiled=True)


def layer_norm(values, gain_vec, bias_vec):
    average = jnp.mean(values, axis=-1, keepdims=True)
    centred = values - average
    variance = jnp.mean(centred * centred, axis=-1, keepdims=True)
    return centred * lax.rsqrt(variance + epsilon) * gain_vec + bias_vec


def projections(pair_rep, mask_float, proj_weight, norm_gain, norm_bias, layer_no):
    channels = pair_rep.shape[2]
    normed = layer_norm(
        pair_rep.astype(jnp.float32), norm_gain[layer_no, 0], norm_bias[layer_no, 0]
    ).astype(jnp.bfloat16)
    flattened = normed.reshape(-1, channels)
    products = [
        jnp.dot(
            flattened, proj_weight[layer_no, which], preferred_element_type=jnp.float32
        ).reshape(pair_rep.shape)
        for which in range(5)
    ]
    left_side = (jax.nn.sigmoid(products[0]) * products[1] * mask_float).astype(jnp.bfloat16)
    right_side = (jax.nn.sigmoid(products[2]) * products[3] * mask_float).astype(jnp.bfloat16)
    gate_value = jax.nn.sigmoid(products[4])
    return (left_side, right_side, gate_value)


def finish(pair_rep, triangle, gate_value, out_weight, norm_gain, norm_bias, layer_no):
    channels = pair_rep.shape[2]
    normed = layer_norm(triangle, norm_gain[layer_no, 1], norm_bias[layer_no, 1]).astype(
        jnp.bfloat16
    )
    projected = jnp.dot(
        normed.reshape(-1, channels), out_weight[layer_no], preferred_element_type=jnp.float32
    ).reshape(pair_rep.shape)
    return (pair_rep.astype(jnp.float32) + gate_value * projected).astype(jnp.bfloat16)


def shards(pair_rep, pair_mask, proj_weight, out_weight, norm_gain, norm_bias):
    rows_dev, cols_dev, channels = pair_rep.shape
    mask_float = pair_mask.astype(jnp.float32)[..., None]
    left_side, right_side, gate_value = projections(
        pair_rep, mask_float, proj_weight, norm_gain, norm_bias, 0
    )
    right_all = lax.all_gather(right_side, "row", axis=0, tiled=True)

    def outgoing_term(first_idx, how_many):
        sliced = lax.dynamic_slice_in_dim(right_all, first_idx, how_many, 0)
        return jnp.einsum("jkc,ikc->jic", sliced, left_side, preferred_element_type=jnp.float32)

    triangle = scattered(outgoing_term, cols_dev, "col")
    triangle = jnp.transpose(triangle, (1, 0, 2))
    pair_rep = finish(pair_rep, triangle, gate_value, out_weight, norm_gain, norm_bias, 0)
    left_side, right_side, gate_value = projections(
        pair_rep, mask_float, proj_weight, norm_gain, norm_bias, 1
    )
    left_all = lax.all_gather(left_side, "col", axis=1, tiled=True)

    def incoming_term(first_idx, how_many):
        sliced = lax.dynamic_slice_in_dim(left_all, first_idx, how_many, 1)
        return jnp.einsum("kic,kjc->ijc", sliced, right_side, preferred_element_type=jnp.float32)

    triangle = scattered(incoming_term, rows_dev, "row")
    pair_rep = finish(pair_rep, triangle, gate_value, out_weight, norm_gain, norm_bias, 1)
    return pair_rep


def solution(mesh):
    in_specs = (P("row", "col", None), P("row", "col"), P(), P(), P(), P())
    out_specs = P("row", "col", None)
    return jax.shard_map(shards, mesh=mesh, in_specs=in_specs, out_specs=out_specs, check_vma=False)
```

profile of v0, /device:TPU:0, one launch (start us, length us, event | category | flops | bytes accessed | tf_op | source)
XLA Modules:
  0.0 137.0 jit_solution(15166773543570996231)
XLA Ops:
  6.5 0.0 reduce-scatter.3.cloned.1.call-start
  6.5 1.0 convert_reduce_fusion
  7.5 1.1 fusion.39
  8.6 0.8 slice_bitcast_fusion
  9.4 1.2 fusion.60
  10.6 1.2 fusion.57
  11.8 0.7 convert_element_type.43
  12.5 1.2 fusion.34
  13.7 1.2 fusion.33
  14.8 11.0 %all_gather.6 = bf16[96,12,128]{2,0,1:T(8,128)(2,1)S(1)} all-gather(bf16[24,12,128]{2,0,1:T(8,128)(2,1)S(1)} %fusion.33), channel_id=1, replica_groups=mesh['row'=4,'col'=8] {'row'}, dimensions={0}, use_global_device_ids=true | all-gather | bytes 368640 | tf_op jit(solution)/shard_map/all_gather | solution.py:56
  25.8 0.4 copy.44
  26.3 0.4 copy.43
  26.7 0.0 copy-start.1
  26.7 0.0 copy-start
  26.7 0.6 convolution_bitcast_fusion
  27.4 1.6 %copy.45 = f32[96,24,128]{2,1,0:T(8,128)} copy(f32[96,24,128]{0,1,2:T(8,128)S(1)} %convolution_bitcast_fusion) | data formatting | bytes 2359296 | tf_op jit(solution)/shard_map/jkc,ikc->jic/transpose | solution.py:60
  28.9 0.0 reduce-scatter.3.cloned.1.call-update
  29.0 0.0 reduce-scatter.5.cloned.1.call-start
  29.0 33.3 %reduce-scatter.3.cloned.1.call-done = f32[12,24,128]{2,1,0:T(8,128)} async-done(((f32[96,24,128]{2,1,0:T(8,128)}), f32[12,24,128]{2,1,0:T(8,128)}) %reduce-scatter.3.cloned.1.call-update) | async-done | bytes 147472 | tf_op jit(solution)/shard_map/reduce_scatter | solution.py:11
  62.3 1.0 bitcast_reduce_fusion
  63.3 1.1 multiply_reduce_fusion.2
  64.5 0.0 copy-done.1
  64.5 1.2 fusion.43
  65.6 0.0 copy-done
  65.7 1.1 fusion.83
  66.8 0.2 multiply_reduce_fusion.1
  67.0 0.1 add_convert_fusion.1
  67.2 0.9 fusion.50
  68.1 0.9 fusion.53
  69.0 1.0 fusion.30
  70.0 1.0 fusion.31
  71.0 1.2 copy.50
  72.2 15.8 %all_gather.7 = bf16[24,96,128]{2,0,1:T(8,128)(2,1)} all-gather(bf16[24,12,128]{2,0,1:T(8,128)(2,1)S(1)} %fusion.30), channel_id=1, replica_groups=mesh['row'=4,'col'=8] {'col'}, dimensions={1}, use_global_device_ids=true | all-gather | bytes 663552 | tf_op jit(solution)/shard_map/all_gather | solution.py:68
  88.0 5.2 %copy.51 = bf16[24,96,128]{0,1,2:T(8,128)(2,1)S(1)} copy(bf16[24,96,128]{2,0,1:T(8,128)(2,1)} %all_gather.7) | data formatting | bytes 1179648 | tf_op jit(solution)/shard_map/all_gather | solution.py:68
  93.3 3.8 %convolution_bitcast_fusion.1 = f32[96,12,128]{0,1,2:T(8,128)} fusion(bf16[24,12,128]{0,1,2:T(8,128)(2,1)} %copy.50, bf16[24,96,128]{0,1,2:T(8,128)(2,1)S(1)} %copy.51), kind=kOutput, calls=%fused_computation.1 | convolution fusion | flops 7077888 | bytes 1253376 | tf_op jit(solution)/shard_map/kic,kjc->ijc/dot_general | solution.py:72
  97.0 2.7 %copy.52 = f32[96,12,128]{2,1,0:T(8,128)} copy(f32[96,12,128]{0,1,2:T(8,128)} %convolution_bitcast_fusion.1) | data formatting | bytes 1179648 | tf_op jit(solution)/shard_map/kic,kjc->ijc/transpose | solution.py:72
  99.7 0.0 reduce-scatter.5.cloned.1.call-update
  99.7 25.0 %reduce-scatter.5.cloned.1.call-done = f32[24,12,128]{2,1,0:T(8,128)} async-done(((f32[96,12,128]{2,1,0:T(8,128)}), f32[24,12,128]{2,1,0:T(8,128)}) %reduce-scatter.5.cloned.1.call-update) | async-done | bytes 147472 | tf_op jit(solution)/shard_map/reduce_scatter | solution.py:11
  124.7 1.0 reduce_sum.78
  125.8 0.1 copy.53
  125.8 0.1 copy.54
  125.9 1.1 multiply_reduce_fusion
  127.1 0.1 copy.55
  127.2 0.1 copy.56
  127.3 1.1 add_convert_fusion
  128.4 0.2 fusion.44
  128.5 1.6 %fusion.32 = bf16[24,12,128]{2,0,1:T(8,128)(2,1)} fusion(f32[24,12,128]{2,0,1:T(8,128)S(1)} %get-tuple-element.14, f32[24,12,128]{2,0,1:T(8,128)S(1)} %fusion.44, bf16[24,12,128]{2,0,1:T(8,128)(2,1)S(1)} %add_convert_fusion.1, bf16[2,5,128,128]{3,2,1,0:T(8,128)(2,1)} %param.8), kind=kOutput, calls=%fused_computation.40 | convolution fusion | flops 9658368 | bytes 475136 | tf_op jit(solution)/shard_map/dot_general | solution.py:28
  (8 shorter events, 0.0 us)
Async XLA Ops:
  6.5 55.8 %reduce-scatter.3.cloned.1.call-start = ((), (), s32[]{:S(2)}) async-start(), calls=%async_computation.2 | async-start | bytes 1327104 | tf_op jit(solution)/shard_map/reduce_scatter | solution.py:11
  26.7 37.8 %copy-start.1 = (bf16[2,128,128]{2,1,0:T(8,128)(2,1)S(1)}, bf16[2,128,128]{2,1,0:T(8,128)(2,1)}, u32[]{:S(2)}) copy-start(bf16[2,128,128]{2,1,0:T(8,128)(2,1)} %param.9) | copy-start | bytes 196612
  26.7 38.9 %copy-start = (bf16[24,12,128]{2,0,1:T(8,128)(2,1)S(1)}, bf16[24,12,128]{2,0,1:T(8,128)(2,1)}, u32[]{:S(2)}) copy-start(bf16[24,12,128]{2,0,1:T(8,128)(2,1)} %param.6) | copy-start | bytes 221188
  29.0 95.7 %reduce-scatter.5.cloned.1.call-start = ((), (), s32[]{:S(2)}) async-start(), calls=%async_computation.3 | async-start | bytes 983040 | tf_op jit(solution)/shard_map/reduce_scatter | solution.py:11
Sparse Core Ops, SparseCore 0:
  29.1 33.1 reduce-scatter.2
  99.9 24.7 reduce-scatter.4
where the time goes:
time: 138 us; the launch traced here: 137 us
  waiting for transfers between devices  58.3 us (42%)
  blocking collectives  26.8 us (19%)
  matrix products  16.9 us (12%)
  between operations  13.6 us (10%)
  local copies, waits for them, and re-layouts  12.7 us (9%)
  other arithmetic  8.57 us (6%)
    reduce_scatter x2, waiting for transfers between devices, scattered(): return lax.psum_scatter(whole, axis, scatter_dimension=0, tiled=True)  58.3 us
    all_gather x1, blocking collectives, shards(): left_all = lax.all_gather(left_side, 'col', axis=1, tiled=True)  15.8 us
    dot_general x10, matrix products, projections(): jnp.dot(flattened, proj_weight[layer_no, which], preferred_element_type=j...  11.2 us
    all_gather x1, blocking collectives, shards(): right_all = lax.all_gather(right_side, 'row', axis=0, tiled=True)  11 us
    all_gather x1, local copies, waits for them, and re-layouts, shards(): left_all = lax.all_gather(left_side, 'col', axis=1, tiled=True)  5.24 us
    dot_general x1, matrix products, incoming_term(): jnp.einsum('kic,kjc->ijc', sliced, right_side, preferred_element_type=jnp...  3.77 us
    reduce_sum x4, other arithmetic, layer_norm(): variance = jnp.mean(centred * centred, axis=-1, keepdims=True)  3.5 us
    reduce_sum x3, other arithmetic, layer_norm(): average = jnp.mean(values, axis=-1, keepdims=True)  3.06 us
  transfers between devices with their start and end apart: 2, of which 2 were waited for; matrix products, arithmetic and copies ran while one was open for 0% of the time, Pallas kernels for 0%

commit v1 on v0

--- a/solution.py
+++ b/solution.py
@@ -65,7 +65,7 @@
     left_side, right_side, gate_value = projections(
         pair_rep, mask_float, proj_weight, norm_gain, norm_bias, 1
     )
-    left_all = lax.all_gather(left_side, "col", axis=1, tiled=True)
+    left_all = jnp.concatenate(lax.all_gather(left_side, "col"), axis=1)
 
     def incoming_term(first_idx, how_many):
         sliced = lax.dynamic_slice_in_dim(left_all, first_idx, how_many, 1)

time: 138 us -> 121 us (0.88)
  matrix products: 16.9 us -> 8.13 us
  local copies, waits for them, and re-layouts: 12.7 us -> 6.11 us
    dot_general x10, matrix products: 11.2 us -> 5.73 us  [projections(): jnp.dot(flattened, proj_weight[layer_no, which], preferred_element_type=j...]
    all_gather x1, local copies, waits for them, and re-layouts: 5.24 us -> 0.06 us  [shards(): left_all = jnp.concatenate(lax.all_gather(left_side, 'col'), axis=1)]
    dot_general x1, matrix products: 3.77 us -> 0.41 us  [incoming_term(): jnp.einsum('kic,kjc->ijc', sliced, right_side, preferred_element_type=jnp...]
where the time goes in v1:
time: 121 us
  waiting for transfers between devices  57.9 us (48%)
  blocking collectives  26.1 us (22%)
  between operations  13.7 us (11%)
  other arithmetic  8.63 us (7%)
  matrix products  8.13 us (7%)
  local copies, waits for them, and re-layouts  6.11 us (5%)
    reduce_scatter x2, waiting for transfers between devices, scattered(): return lax.psum_scatter(whole, axis, scatter_dimension=0, tiled=True)  57.9 us
    all_gather x1, blocking collectives, shards(): left_all = jnp.concatenate(lax.all_gather(left_side, 'col'), axis=1)  15.1 us
    all_gather x1, blocking collectives, shards(): right_all = lax.all_gather(right_side, 'row', axis=0, tiled=True)  11 us
    dot_general x10, matrix products, projections(): jnp.dot(flattened, proj_weight[layer_no, which], preferred_element_type=j...  5.73 us
    reduce_sum x4, other arithmetic, layer_norm(): variance = jnp.mean(centred * centred, axis=-1, keepdims=True)  3.5 us
    reduce_sum x3, other arithmetic, layer_norm(): average = jnp.mean(values, axis=-1, keepdims=True)  3.12 us
  transfers between devices with their start and end apart: 2, of which 2 were waited for; matrix products, arithmetic and copies ran while one was open for 0% of the time, Pallas kernels for 0%

profile of v1, /device:TPU:0, one launch (start us, length us, event | category | flops | bytes accessed | tf_op | source)
XLA Modules:
  0.0 120.6 jit_solution(4517147775157252490)
XLA Ops:
  6.5 0.0 copy-start
  6.5 0.0 copy-start.2
  6.5 0.0 reduce-scatter.3.cloned.1.call-start
  6.5 1.1 convert_reduce_fusion
  7.6 1.1 fusion.39
  8.7 0.8 slice_bitcast_fusion
  9.5 1.2 fusion.60
  10.7 1.2 fusion.57
  11.8 0.7 convert_element_type.43
  12.5 1.2 fusion.34
  13.7 0.0 copy-done
  13.7 0.0 copy-done.2
  13.7 0.3 fusion.33
  14.0 11.0 %all_gather.9 = bf16[96,12,128]{2,0,1:T(8,128)(2,1)S(1)} all-gather(bf16[24,12,128]{2,0,1:T(8,128)(2,1)S(1)} %fusion.33), channel_id=1, replica_groups=mesh['row'=4,'col'=8] {'row'}, dimensions={0}, use_global_device_ids=true | all-gather | bytes 368640 | tf_op jit(solution)/shard_map/all_gather | solution.py:56
  25.0 0.4 copy.55
  25.5 0.4 copy.54
  25.9 0.6 convolution_bitcast_fusion
  26.6 0.0 copy-start.1
  26.6 1.6 %copy.56 = f32[96,24,128]{2,1,0:T(8,128)} copy(f32[96,24,128]{0,1,2:T(8,128)S(1)} %convolution_bitcast_fusion) | data formatting | bytes 2359296 | tf_op jit(solution)/shard_map/jkc,ikc->jic/transpose | solution.py:60
  28.1 0.0 reduce-scatter.3.cloned.1.call-update
  28.1 0.0 reduce-scatter.5.cloned.1.call-start
  28.2 33.3 %reduce-scatter.3.cloned.1.call-done = f32[12,24,128]{2,1,0:T(8,128)} async-done(((f32[96,24,128]{2,1,0:T(8,128)}), f32[12,24,128]{2,1,0:T(8,128)}) %reduce-scatter.3.cloned.1.call-update) | async-done | bytes 147472 | tf_op jit(solution)/shard_map/reduce_scatter | solution.py:11
  61.5 1.0 bitcast_reduce_fusion
  62.6 1.1 multiply_reduce_fusion.2
  63.7 0.0 copy-done.1
  63.7 1.2 fusion.43
  64.9 0.4 fusion.83
  65.3 0.2 multiply_reduce_fusion.1
  65.5 0.1 add_convert_fusion.1
  65.6 0.2 fusion.50
  65.8 0.2 fusion.53
  66.0 0.2 fusion.30
  66.2 0.2 fusion.31
  66.4 0.4 copy.62
  66.8 15.1 %all-gather = bf16[192,12,128]{2,0,1:T(8,128)(2,1)S(1)} all-gather(bf16[24,12,128]{2,0,1:T(8,128)(2,1)S(1)} %fusion.30), channel_id=2, replica_groups=mesh['row'=4,'col'=8] {'col'}, dimensions={0}, use_global_device_ids=true | all-gather | bytes 663552 | tf_op jit(solution)/shard_map/all_gather | solution.py:68
  82.0 0.1 copy.61
  82.0 0.6 copy.63
  82.6 0.4 convolution_bitcast_fusion.1
  83.0 1.5 %copy.64 = f32[96,12,128]{2,1,0:T(8,128)} copy(f32[96,12,128]{0,1,2:T(8,128)S(1)} %convolution_bitcast_fusion.1) | data formatting | bytes 1179648 | tf_op jit(solution)/shard_map/kic,kjc->ijc/transpose | solution.py:72
  84.5 0.0 reduce-scatter.5.cloned.1.call-update
  84.5 24.6 %reduce-scatter.5.cloned.1.call-done = f32[24,12,128]{2,1,0:T(8,128)} async-done(((f32[96,12,128]{2,1,0:T(8,128)}), f32[24,12,128]{2,1,0:T(8,128)}) %reduce-scatter.5.cloned.1.call-update) | async-done | bytes 147472 | tf_op jit(solution)/shard_map/reduce_scatter | solution.py:11
  109.1 1.0 reduce_sum.78
  110.2 0.1 copy.65
  110.2 0.1 copy.66
  110.3 1.1 multiply_reduce_fusion
  111.5 0.1 copy.67
  111.6 0.1 copy.68
  111.7 1.1 add_convert_fusion
  112.8 0.2 fusion.44
  112.9 0.8 fusion.32
  (8 shorter events, 0.0 us)
Async XLA Ops:
  6.5 7.2 %copy-start = (bf16[24,12,128]{2,0,1:T(8,128)(2,1)S(1)}, bf16[24,12,128]{2,0,1:T(8,128)(2,1)}, u32[]{:S(2)}) copy-start(bf16[24,12,128]{2,0,1:T(8,128)(2,1)} %param.6) | copy-start | bytes 221188
  6.5 7.2 %copy-start.2 = (bf16[2,5,128,128]{3,2,1,0:T(8,128)(2,1)S(1)}, bf16[2,5,128,128]{3,2,1,0:T(8,128)(2,1)}, u32[]{:S(2)}) copy-start(bf16[2,5,128,128]{3,2,1,0:T(8,128)(2,1)} %param.8) | copy-start | bytes 983044
  6.5 55.0 %reduce-scatter.3.cloned.1.call-start = ((), (), s32[]{:S(2)}) async-start(), calls=%async_computation.2 | async-start | bytes 1327104 | tf_op jit(solution)/shard_map/reduce_scatter | solution.py:11
  26.6 37.1 %copy-start.1 = (bf16[2,128,128]{2,1,0:T(8,128)(2,1)S(1)}, bf16[2,128,128]{2,1,0:T(8,128)(2,1)}, u32[]{:S(2)}) copy-start(bf16[2,128,128]{2,1,0:T(8,128)(2,1)} %param.9) | copy-start | bytes 196612
  28.1 81.0 %reduce-scatter.5.cloned.1.call-start = ((), (), s32[]{:S(2)}) async-start(), calls=%async_computation.3 | async-start | bytes 983040 | tf_op jit(solution)/shard_map/reduce_scatter | solution.py:11
Sparse Core Ops, SparseCore 0:
  28.3 33.2 reduce-scatter.2
  84.6 24.4 reduce-scatter.4
